TPU v7x, 32 devices: a whole 2x2x4 slice. The times are simulated.
32 devices in a mesh: dp: 2 (over x), expert: 4 (over y, core), sample: 4 (over z).
Axes of the slice: x: 2, y: 2, z: 4, core: 2. Of those that a mesh axis runs over, the one named last changes fastest.
Arguments:
- tokens: bfloat16 [640, 4096], P(('dp', 'expert', 'sample')), may hold values from -6 to 6
- cotangent: bfloat16 [640, 4096], P(('dp', 'expert', 'sample')), may hold values from -6 to 6
- routes: int32 [640, 2], P(('dp', 'expert', 'sample')), may hold values from 0 to 7, all different within a row; in each aligned block of 20 rows (0 to 19, 20 to 39, ...) at most 6 rows name the same one
- gate_weights: float32 [640, 2], P(('dp', 'expert', 'sample')), may hold values from 0.1 to 1
- lengths: int32 [8, 4], P(('dp', 'expert'), 'sample'), may hold values from 1 to 20
- rewards: int32 [8, 4], P(('dp', 'expert'), 'sample'), may hold values from -48 to 48
- w_gate: bfloat16 [8, 8192, 4096], P('expert', ('dp', 'sample')), may hold values from -0.09375 to 0.09375
- w_up: bfloat16 [8, 8192, 4096], P('expert', ('dp', 'sample')), may hold values from -0.09375 to 0.09375
- w_down: bfloat16 [8, 8192, 4096], P('expert', ('dp', 'sample')), may hold values from -0.0625 to 0.0625
Outputs:
- grad_tokens: bfloat16 [640, 4096], P(('dp', 'expert', 'sample'))
- grad_w_gate: bfloat16 [8, 8192, 4096], P('expert', ('dp', 'sample'))
- grad_w_up: bfloat16 [8, 8192, 4096], P('expert', ('dp', 'sample'))
- grad_w_down: bfloat16 [8, 8192, 4096], P('expert', ('dp', 'sample'))
Inputs may be any that keep to these rules, and one draw needn't show every extreme that they name: `routes`: each row names 2 different experts; among the rows of one device no expert is named by more than 6 rows, and in every draw some device's rows name some expert exactly 6 times.
All inputs are finite; a program needn't handle non-finite values.
Results may differ from a plain program's by a relative error of at most 0.025.
Values may be sent and summed in bfloat16 or wider, within the bound.
A program may use at most 192 MiB of HBM per device.

v0:
```python
import jax
import jax.numpy as jnp
from jax import lax
from jax.sharding import PartitionSpec as P

CAP = 6


def silu_parts(pre_gate):
    gate_prob = jax.nn.sigmoid(pre_gate)
    return (pre_gate * gate_prob, gate_prob * (1.0 + pre_gate * (1.0 - gate_prob)))


def expert_rows(inputs, grads_out, w_gate, w_up, w_down):
    pre_gate = jnp.einsum("rjcd,jfd->rjcf", inputs, w_gate, preferred_element_type=jnp.float32)
    pre_up = jnp.einsum("rjcd,jfd->rjcf", inputs, w_up, preferred_element_type=jnp.float32)
    active, derivative = silu_parts(pre_gate)
    hidden = (active * pre_up).astype(jnp.bfloat16)
    grad_hidden = jnp.einsum(
        "rjcd,jfd->rjcf", grads_out, w_down, preferred_element_type=jnp.float32
    )
    grad_gate = (grad_hidden * pre_up * derivative).astype(jnp.bfloat16)
    grad_up = (grad_hidden * active).astype(jnp.bfloat16)
    return (hidden, grad_gate, grad_up)


def weight_terms(inputs, grads_out, hidden, grad_gate, grad_up):
    term_gate = jnp.einsum("rjcf,rjcd->jfd", grad_gate, inputs, preferred_element_type=jnp.float32)
    term_up = jnp.einsum("rjcf,rjcd->jfd", grad_up, inputs, preferred_element_type=jnp.float32)
    term_down = jnp.einsum("rjcf,rjcd->jfd", hidden, grads_out, preferred_element_type=jnp.float32)
    return (term_gate, term_up, term_down)


def input_terms(grad_gate, grad_up, w_gate, w_up):
    from_gate = jnp.einsum("rjcf,jfd->rjcd", grad_gate, w_gate, preferred_element_type=jnp.float32)
    from_up = jnp.einsum("rjcf,jfd->rjcd", grad_up, w_up, preferred_element_type=jnp.float32)
    return from_gate + from_up


def local(tokens, cotangent, routes, gate_weights, lengths, rewards, w_gate, w_up, w_down):
    samples = lax.axis_size("sample")
    own_reward = rewards.astype(jnp.float32) * 0.0625
    reward_total = lax.psum(own_reward, "sample")
    advantage = own_reward - (reward_total - own_reward) / (samples - 1)
    token_count = tokens.shape[0]
    model_width = tokens.shape[1]
    choices_per = routes.shape[1]
    local_experts = w_gate.shape[0]
    expert_groups = lax.axis_size("expert")
    all_experts = local_experts * expert_groups
    positions = jnp.arange(token_count, dtype=jnp.int32)
    weight_row = jnp.where(positions < lengths[0, 0], -advantage[0, 0], jnp.zeros((), jnp.float32))
    pair_scale = (gate_weights * weight_row[:, None]).reshape(-1)
    pair_expert = routes.reshape(-1)
    member = (pair_expert[:, None] == jnp.arange(all_experts, dtype=jnp.int32)[None, :]).astype(
        jnp.int32
    )
    earlier = jnp.sum((jnp.cumsum(member, axis=0) - member) * member, axis=1)
    target = pair_expert * CAP + earlier
    slot_ids = jnp.arange(all_experts * CAP, dtype=jnp.int32)
    placed = target[:, None] == slot_ids[None, :]
    chosen = jnp.sum(
        placed.reshape(token_count, choices_per, -1).astype(jnp.float32), axis=1
    ).astype(jnp.bfloat16)
    slot_scale = jnp.sum(jnp.where(placed, pair_scale[:, None], jnp.zeros((), jnp.float32)), axis=0)
    sent_inputs = jnp.dot(chosen.T, tokens, preferred_element_type=jnp.float32).astype(jnp.bfloat16)
    sent_cotangent = jnp.dot(chosen.T, cotangent, preferred_element_type=jnp.float32)
    sent_grads = (sent_cotangent * slot_scale[:, None]).astype(jnp.bfloat16)
    layout = (expert_groups, local_experts, CAP, model_width)
    arrived_inputs, arrived_grads = (
        lax.all_to_all(
            sent_inputs.reshape(layout), "expert", split_axis=0, concat_axis=0, tiled=True
        ),
        lax.all_to_all(
            sent_grads.reshape(layout), "expert", split_axis=0, concat_axis=0, tiled=True
        ),
    )
    group_inputs, group_grads = (
        lax.all_gather(arrived_inputs, ("dp", "sample"), axis=0, tiled=True),
        lax.all_gather(arrived_grads, ("dp", "sample"), axis=0, tiled=True),
    )
    hidden, grad_gate, grad_up = expert_rows(group_inputs, group_grads, w_gate, w_up, w_down)
    term_gate, term_up, term_down = weight_terms(
        group_inputs, group_grads, hidden, grad_gate, grad_up
    )
    row_sums = lax.psum_scatter(
        input_terms(grad_gate, grad_up, w_gate, w_up).astype(jnp.bfloat16),
        ("dp", "sample"),
        scatter_dimension=0,
        tiled=True,
    )
    returned = lax.all_to_all(row_sums, "expert", split_axis=0, concat_axis=0, tiled=True)
    flat_back = returned.reshape(all_experts * CAP, model_width)
    grad_tokens = jnp.dot(chosen, flat_back, preferred_element_type=jnp.float32).astype(
        jnp.bfloat16
    )
    return (
        grad_tokens,
        term_gate.astype(jnp.bfloat16),
        term_up.astype(jnp.bfloat16),
        term_down.astype(jnp.bfloat16),
    )


def solution(mesh):
    in_specs = (
        P(("dp", "expert", "sample"), None),
        P(("dp", "expert", "sample"), None),
        P(("dp", "expert", "sample"), None),
        P(("dp", "expert", "sample"), None),
        P(("dp", "expert"), "sample"),
        P(("dp", "expert"), "sample"),
        P("expert", ("dp", "sample"), None),
        P("expert", ("dp", "sample"), None),
        P("expert", ("dp", "sample"), None),
    )
    out_specs = (
        P(("dp", "expert", "sample"), None),
        P("expert", ("dp", "sample"), None),
        P("expert", ("dp", "sample"), None),
        P("expert", ("dp", "sample"), None),
    )
    return jax.shard_map(local, mesh=mesh, in_specs=in_specs, out_specs=out_specs, check_vma=False)
```

profile of v0, /device:TPU:0, one launch (start us, length us, event | category | flops | bytes accessed | tf_op | source)
XLA Modules:
  0.0 334.2 jit_solution(651545220451773248)
XLA Ops:
  7.2 0.0 copy-start
  7.2 0.0 all-gather.5.cloned.1.call-start
  7.2 0.9 copy.67
  8.1 0.1 eq.35
  8.2 0.1 fusion.33
  8.3 0.1 reduce_window_sum.11
  8.4 0.2 select_reduce_fusion.1
  8.6 0.1 reduce_sum.30
  8.7 0.1 copy.68
  8.8 0.7 multiply_add_fusion
  9.4 0.1 copy.69
  9.5 0.1 fusion.32
  9.7 0.3 convolution_convert_fusion
  10.0 0.0 copy-start.7
  10.0 0.1 reshape.46
  10.1 0.4 copy.73
  10.5 11.6 %all_to_all.15 = bf16[4,2,6,4096]{3,1,2,0:T(2,128)(2,1)} all-to-all(bf16[4,2,6,4096]{3,1,2,0:T(2,128)(2,1)S(1)} %copy.73), channel_id=1, replica_groups=mesh['dp'=2,'expert'=4,'sample'=4] {'expert'}, dimensions={0} | all-to-all | bytes 786432 | tf_op jit(solution)/shard_map/all_to_all | solution.py:71
  22.1 0.0 all-gather.5.cloned.1.call-update
  22.1 0.0 all-gather.3.cloned.1.call-start
  22.8 13.1 %psum.7 = f32[1,1]{1,0:T(1,128)} all-reduce(f32[1,1]{1,0:T(1,128)S(6)} %mul.63), channel_id=1, replica_groups=mesh['dp'=2,'expert'=4,'sample'=4] {'sample'}, use_global_device_ids=true, to_apply=%region_3.4 | all-reduce | flops 1 | bytes 8 | tf_op jit(solution)/shard_map/psum | solution.py:43
  37.2 0.1 copy.70
  37.3 0.1 broadcast_in_dim.29
  37.4 0.1 select_reduce_fusion
  37.5 0.3 fusion.15
  37.8 0.1 reshape.45
  38.0 0.4 copy.71
  38.4 10.5 %all_to_all.16 = bf16[4,2,6,4096]{3,1,2,0:T(2,128)(2,1)} all-to-all(bf16[4,2,6,4096]{3,1,2,0:T(2,128)(2,1)S(1)} %copy.71), channel_id=1, replica_groups=mesh['dp'=2,'expert'=4,'sample'=4] {'expert'}, dimensions={0} | all-to-all | bytes 786432 | tf_op jit(solution)/shard_map/all_to_all | solution.py:74
  48.9 0.0 all-gather.3.cloned.1.call-update
  48.9 0.6 all-reduce.3.cloned.1.call-start
  49.5 0.6 dynamic-slice
  50.7 32.3 %all-gather.5.cloned.1.call-done = bf16[32,2,6,4096]{3,1,2,0:T(2,128)(2,1)} async-done(((bf16[4,2,6,4096]{3,1,2,0:T(2,128)(2,1)}), bf16[32,2,6,4096]{3,1,2,0:T(2,128)(2,1)}) %all-gather.5.cloned.1.call-update) | async-done | bytes 3145744 | tf_op jit(solution)/shard_map/all_gather | solution.py:79
  83.0 15.3 %fusion.2 = f32[2,32,6,1024]{3,1,2,0:T(8,128)} fusion(bf16[2,1024,4096]{2,1,0:T(8,128)(2,1)} %param.15, bf16[32,2,6,4096]{3,1,2,0:T(2,128)(2,1)} %all-gather.5.cloned.1.call-done), kind=kOutput, calls=%fused_computation.5 | convolution fusion | flops 3221225472 | bytes 21495808 | tf_op jit(solution)/shard_map/rjcd,jfd->rjcf/dot_general | solution.py:15
  98.3 14.6 %fusion.8 = f32[2,32,6,1024]{3,1,2,0:T(8,128)} fusion(bf16[2,1024,4096]{2,1,0:T(8,128)(2,1)} %param.16, bf16[32,2,6,4096]{3,1,2,0:T(2,128)(2,1)S(1)} %copy-done.6), kind=kOutput, calls=%fused_computation.11 | convolution fusion | flops 3221225472 | bytes 21495808 | tf_op jit(solution)/shard_map/rjcd,jfd->rjcf/dot_general | solution.py:16
  112.9 30.9 %all-gather.3.cloned.1.call-done = bf16[32,2,6,4096]{3,1,2,0:T(2,128)(2,1)} async-done(((bf16[4,2,6,4096]{3,1,2,0:T(2,128)(2,1)}), bf16[32,2,6,4096]{3,1,2,0:T(2,128)(2,1)}) %all-gather.3.cloned.1.call-update) | async-done | bytes 3145744 | tf_op jit(solution)/shard_map/all_gather | solution.py:80
  143.8 15.0 %fusion.30 = (bf16[32,2,6,1024]{3,0,2,1:T(8,128)(2,1)S(1)}, bf16[32,2,6,1024]{3,0,2,1:T(8,128)(2,1)S(1)}) fusion(f32[2,32,6,1024]{3,1,2,0:T(8,128)} %fusion.2, f32[2,32,6,1024]{3,1,2,0:T(8,128)} %fusion.8, bf16[2,1024,4096]{2,1,0:T(8,128)(2,1)} %param.17, bf16[32,2,6,4096]{3,1,2,0:T(2,128)(2,1)} %all-gather.3.cloned.1.call-done), kind=kOutput, calls=%fused_computation.39 | convolution fusion | flops 3226337280 | bytes 24641536 | tf_op jit(solution)/shard_map/rjcd,jfd->rjcf/dot_general | solution.py:19
  158.9 7.6 %fusion = f32[2,32,6,4096]{3,1,2,0:T(8,128)S(1)} fusion(bf16[32,2,6,1024]{3,0,2,1:T(8,128)(2,1)S(1)} %get-tuple-element.5, bf16[2,1024,4096]{2,1,0:T(8,128)(2,1)} %param.15), kind=kOutput, calls=%fused_computation.3 | convolution fusion | flops 3221225472 | bytes 23855104 | tf_op jit(solution)/shard_map/rjcf,jfd->rjcd/dot_general | solution.py:35
  166.5 11.1 %fusion.12 = bf16[32,2,6,4096]{3,0,2,1:T(8,128)(2,1)} fusion(f32[2,32,6,4096]{3,1,2,0:T(8,128)S(1)} %fusion, bf16[32,2,6,1024]{3,0,2,1:T(8,128)(2,1)S(1)} %get-tuple-element.4, bf16[2,1024,4096]{2,1,0:T(8,128)(2,1)} %param.16), kind=kOutput, calls=%fused_computation.14 | convolution fusion | flops 3224371200 | bytes 27000832 | tf_op jit(solution)/shard_map/rjcf,jfd->rjcd/dot_general | solution.py:36
  177.6 0.0 all-reduce.3.cloned.1.call-update
  177.6 14.9 %bitcast_convert_fusion.1 = bf16[2,1024,4096]{2,1,0:T(8,128)(2,1)} fusion(bf16[32,2,6,1024]{3,0,2,1:T(8,128)(2,1)S(1)} %get-tuple-element.4, bf16[32,2,6,4096]{3,1,2,0:T(2,128)(2,1)} %all-gather.5.cloned.1.call-done), kind=kOutput, calls=%fused_computation.1 | convolution fusion | flops 3229614080 | bytes 20709376 | tf_op jit(solution)/shard_map/rjcf,rjcd->jfd/dot_general | solution.py:29
  192.6 15.1 %bitcast_convert_fusion = bf16[2,1024,4096]{2,1,0:T(8,128)(2,1)} fusion(bf16[32,2,6,4096]{3,1,2,0:T(2,128)(2,1)} %all-gather.3.cloned.1.call-done, f32[2,32,6,1024]{3,1,2,0:T(8,128)} %fusion.8, f32[2,32,6,1024]{3,1,2,0:T(8,128)S(1)} %copy-done.8), kind=kOutput, calls=%fused_computation | convolution fusion | flops 3231973376 | bytes 23068672 | tf_op jit(solution)/shard_map/rjcf,rjcd->jfd/dot_general | solution.py:30
  207.7 97.6 %all-reduce.3.cloned.1.call-done = bf16[32,2,6,4096]{3,0,2,1:T(8,128)(2,1)} async-done(((bf16[32,2,6,4096]{3,0,2,1:T(8,128)(2,1)}), bf16[32,2,6,4096]{3,0,2,1:T(8,128)(2,1)}) %all-reduce.3.cloned.1.call-update) | async-done | bytes 3145744
  305.2 1.4 constant_dynamic-slice_fusion
  306.6 1.2 copy.76
  307.7 3.7 %all-to-all-start.2 = ((bf16[4,2,6,4096]{3,1,2,0:T(2,128)(2,1)}), bf16[4,2,6,4096]{3,1,2,0:T(2,128)(2,1)S(1)}, u32[]{:S(2)}, u32[]{:S(2)}) async-start(bf16[4,2,6,4096]{3,1,2,0:T(2,128)(2,1)} %copy.76), calls=%async_computation.2 | async-start | bytes 786432 | tf_op jit(solution)/shard_map/all_to_all | solution.py:92
  311.5 14.7 %bitcast_convert_fusion.2 = bf16[2,1024,4096]{2,1,0:T(8,128)(2,1)} fusion(bf16[32,2,6,1024]{3,0,2,1:T(8,128)(2,1)S(1)} %get-tuple-element.5, bf16[32,2,6,4096]{3,1,2,0:T(2,128)(2,1)} %all-gather.5.cloned.1.call-done), kind=kOutput, calls=%fused_computation.2 | convolution fusion | flops 3229614080 | bytes 20709376 | tf_op jit(solution)/shard_map/rjcf,rjcd->jfd/dot_general | solution.py:28
  326.1 0.2 copy.77
  326.4 0.1 reshape.47
  326.5 0.9 convolution_convert_fusion.1
  (20 shorter events, 0.1 us)
Async XLA Ops:
  7.2 2.5 copy-start
  7.2 30.0 %copy-start.5 = (f32[20,2]{0,1:T(2,128)S(1)}, f32[20,2]{0,1:T(2,128)}, u32[]{:S(2)}) copy-start(f32[20,2]{0,1:T(2,128)} %param.12) | copy-start | bytes 484
  7.2 30.4 %copy-start.2 = (bf16[20,4096]{1,0:T(8,128)(2,1)S(1)}, bf16[20,4096]{1,0:T(8,128)(2,1)}, u32[]{:S(2)}) copy-start(bf16[20,4096]{1,0:T(8,128)(2,1)} %param.10) | copy-start | bytes 491524
  7.2 75.8 %all-gather.5.cloned.1.call-start = ((), (), s32[]{:S(2)}) async-start(), calls=%async_computation.4 | async-start | bytes 3538944 | tf_op jit(solution)/shard_map/all_gather | solution.py:79
  9.7 39.2 %copy-start.3 = (bf16[20,48]{1,0:T(8,128)(2,1)}, bf16[20,48]{1,0:T(8,128)(2,1)S(1)}, u32[]{:S(2)}) copy-start(bf16[20,48]{1,0:T(8,128)(2,1)S(1)} %fusion.32) | copy-start | bytes 5764
  10.0 39.5 %copy-start.7 = (u32[32]{0:T(128)S(1)}, u32[32]{0:T(128)}, u32[]{:S(2)}) copy-start(u32[32]{0:T(128)} %constant.28) | copy-start | bytes 388
  22.1 121.7 %all-gather.3.cloned.1.call-start = ((), (), s32[]{:S(2)}) async-start(), calls=%async_computation.3 | async-start | bytes 3538944 | tf_op jit(solution)/shard_map/all_gather | solution.py:80
  48.9 256.3 %all-reduce.3.cloned.1.call-start = ((), (), s32[]{:S(2)}) async-start(), calls=%async_computation.5 | async-start | bytes 6291456
  83.0 15.3 %copy-start.6 = (bf16[32,2,6,4096]{3,1,2,0:T(2,128)(2,1)S(1)}, bf16[32,2,6,4096]{3,1,2,0:T(2,128)(2,1)}, u32[]{:S(2)}) copy-start(bf16[32,2,6,4096]{3,1,2,0:T(2,128)(2,1)} %all-gather.5.cloned.1.call-done) | copy-start | bytes 9437188
  177.6 14.9 %copy-start.8 = (f32[2,32,6,1024]{3,1,2,0:T(8,128)S(1)}, f32[2,32,6,1024]{3,1,2,0:T(8,128)}, u32[]{:S(2)}) copy-start(f32[2,32,6,1024]{3,1,2,0:T(8,128)} %fusion.2) | copy-start | bytes 4718596
  307.7 18.4 %all-to-all-start.2 = ((bf16[4,2,6,4096]{3,1,2,0:T(2,128)(2,1)}), bf16[4,2,6,4096]{3,1,2,0:T(2,128)(2,1)S(1)}, u32[]{:S(2)}, u32[]{:S(2)}) async-start(bf16[4,2,6,4096]{3,1,2,0:T(2,128)(2,1)} %copy.76), calls=%async_computation.2 | async-start | bytes 786432 | tf_op jit(solution)/shard_map/all_to_all | solution.py:92
  311.5 15.1 %copy-start.4 = (bf16[20,48]{1,0:T(8,128)(2,1)S(1)}, bf16[20,48]{1,0:T(8,128)(2,1)}, u32[]{:S(2)}) copy-start(bf16[20,48]{1,0:T(8,128)(2,1)} %copy-done.3) | copy-start | bytes 5764
  311.5 15.9 %copy-start.1 = (bf16[20,4096]{1,0:T(8,128)(2,1)S(1)}, bf16[20,4096]{1,0:T(8,128)(2,1)}, u32[]{:S(2)}) copy-start(bf16[20,4096]{1,0:T(8,128)(2,1)} %param.9) | copy-start | bytes 491524
Sparse Core Ops, SparseCore 0:
  22.3 60.7 all-gather.4
  85.1 58.6 all-gather.2
  177.8 127.4 all-reduce.2
where the time goes:
time: 337 us; the launch traced here: 334 us
  waiting for transfers between devices  161 us (48%)
  matrix products  110 us (33%)
  blocking collectives  35.1 us (10%)
  between operations  16.9 us (5%)
  local copies, waits for them, and re-layouts  6.05 us (2%)
  starting transfers between devices  4.36 us (1%)
    unnamed x4, waiting for transfers between devices  97.6 us
    all_gather x1, waiting for transfers between devices, local(): lax.all_gather(arrived_inputs, ('dp', 'sample'), axis=0, tiled=True)  32.3 us
    all_gather x1, waiting for transfers between devices, local(): lax.all_gather(arrived_grads, ('dp', 'sample'), axis=0, tiled=True)  30.9 us
    dot_general x1, matrix products, expert_rows(): jnp.einsum('rjcd,jfd->rjcf', inputs, w_gate, preferred_element_type=jnp.f...  15.3 us
    dot_general x1, matrix products, weight_terms(): jnp.einsum('rjcf,rjcd->jfd', hidden, grads_out, preferred_element_type=jn...  15.1 us
    dot_general x1, matrix products, expert_rows(): jnp.einsum('rjcd,jfd->rjcf', grads_out, w_down, preferred_element_type=jn...  15 us
    dot_general x1, matrix products, weight_terms(): jnp.einsum('rjcf,rjcd->jfd', grad_up, inputs, preferred_element_type=jnp....  14.9 us
    dot_general x1, matrix products, weight_terms(): jnp.einsum('rjcf,rjcd->jfd', grad_gate, inputs, preferred_element_type=jn...  14.7 us
  transfers between devices with their start and end apart: 4, of which 3 were waited for; matrix products, arithmetic and copies ran while one was open for 23% of the time, Pallas kernels for 0%

commit v1 on v0

--- a/solution.py
+++ b/solution.py
@@ -37,10 +37,24 @@
     return from_gate + from_up
 
 
+def send_sum(blocks, axis):
+    count = lax.axis_size(axis)
+    me = lax.axis_index(axis)
+    total = lax.dynamic_index_in_dim(blocks, me, 0, keepdims=False).astype(jnp.float32)
+    for step in range(1, count):
+        outgoing = lax.dynamic_index_in_dim(blocks, (me + step) % count, 0, keepdims=False)
+        perm = [(i, (i + step) % count) for i in range(count)]
+        total = total + lax.ppermute(outgoing, axis, perm).astype(jnp.float32)
+    return total.astype(jnp.bfloat16)
+
+
 def local(tokens, cotangent, routes, gate_weights, lengths, rewards, w_gate, w_up, w_down):
     samples = lax.axis_size("sample")
     own_reward = rewards.astype(jnp.float32) * 0.0625
-    reward_total = lax.psum(own_reward, "sample")
+    reward_total = own_reward
+    for step in range(1, samples):
+        perm = [(i, (i + step) % samples) for i in range(samples)]
+        reward_total = reward_total + lax.ppermute(own_reward, "sample", perm)
     advantage = own_reward - (reward_total - own_reward) / (samples - 1)
     token_count = tokens.shape[0]
     model_width = tokens.shape[1]
@@ -83,12 +97,10 @@
     term_gate, term_up, term_down = weight_terms(
         group_inputs, group_grads, hidden, grad_gate, grad_up
     )
-    row_sums = lax.psum_scatter(
-        input_terms(grad_gate, grad_up, w_gate, w_up).astype(jnp.bfloat16),
-        ("dp", "sample"),
-        scatter_dimension=0,
-        tiled=True,
-    )
+    parts = input_terms(grad_gate, grad_up, w_gate, w_up).astype(jnp.bfloat16)
+    dp_size = lax.axis_size("dp")
+    parts = parts.reshape(dp_size, samples, all_experts * CAP, model_width)
+    row_sums = send_sum(send_sum(parts, "dp"), "sample").reshape(layout)
     returned = lax.all_to_all(row_sums, "expert", split_axis=0, concat_axis=0, tiled=True)
     flat_back = returned.reshape(all_experts * CAP, model_width)
     grad_tokens = jnp.dot(chosen, flat_back, preferred_element_type=jnp.float32).astype(

time: 337 us -> 290 us (0.86)
  waiting for transfers between devices: 161 us -> 108 us
  starting transfers between devices: 4.36 us -> 18.2 us
  blocking collectives: 35.1 us -> 22.1 us
  local copies, waits for them, and re-layouts: 6.05 us -> 14.7 us
  matrix products: 110 us -> 103 us
    unnamed x4 -> x2, waiting for transfers between devices: 97.6 us -> 0.03 us
    ppermute x0 -> x7, waiting for transfers between devices: none -> 42.3 us  [the longest x4 39.8 us: send_sum(): total = total + lax.ppermute(outgoing, axis, perm).astype(jnp.float32)]
    ppermute x0 -> x7, starting transfers between devices: none -> 14.7 us  [the longest x3 8.95 us: local(): reward_total = reward_total + lax.ppermute(own_reward, 'sample', perm)]
    psum x1 -> x0, blocking collectives: 13.1 us -> none  [local(): reward_total = lax.psum(own_reward, 'sample')]
    reshape x0 -> x3, local copies, waits for them, and re-layouts: none -> 5.46 us  [the longest x1 4.15 us: local(): parts = parts.reshape(dp_size, samples, all_experts * CAP, model_width)]
    dot_general x1, matrix products: 15.1 us -> 11 us  [weight_terms(): jnp.einsum('rjcf,rjcd->jfd', hidden, grads_out, preferred_element_type=jn...]
    convert_element_type x0 -> x1, local copies, waits for them, and re-layouts: none -> 3.77 us  [local(): parts = input_terms(grad_gate, grad_up, w_gate, w_up).astype(jnp.bfloat16)]
  transfers between devices with their start and end apart: 4 -> 10, of which waited for: 3 -> 6; matrix products, arithmetic and copies ran while one was open for 23% -> 24% of each run, Pallas kernels for 0% -> 0%
where the time goes in v1:
time: 290 us; the launch traced here: 287 us
  waiting for transfers between devices  108 us (37%)
  matrix products  103 us (36%)
  blocking collectives  22.1 us (8%)
  starting transfers between devices  18.2 us (6%)
  between operations  17.9 us (6%)
  local copies, waits for them, and re-layouts  14.7 us (5%)
  other arithmetic  2.96 us (1%)
    ppermute x4, waiting for transfers between devices, send_sum(): total = total + lax.ppermute(outgoing, axis, perm).astype(jnp.float32)  39.8 us
    all_gather x1, waiting for transfers between devices, local(): lax.all_gather(arrived_inputs, ('dp', 'sample'), axis=0, tiled=True)  34.4 us
    all_gather x1, waiting for transfers between devices, local(): lax.all_gather(arrived_grads, ('dp', 'sample'), axis=0, tiled=True)  31 us
    dot_general x1, matrix products, expert_rows(): jnp.einsum('rjcd,jfd->rjcf', inputs, w_gate, preferred_element_type=jnp.f...  15.3 us
    dot_general x1, matrix products, expert_rows(): jnp.einsum('rjcd,jfd->rjcf', grads_out, w_down, preferred_element_type=jn...  15 us
    dot_general x1, matrix products, weight_terms(): jnp.einsum('rjcf,rjcd->jfd', grad_gate, inputs, preferred_element_type=jn...  14.7 us
    dot_general x1, matrix products, expert_rows(): jnp.einsum('rjcd,jfd->rjcf', inputs, w_up, preferred_element_type=jnp.flo...  14.6 us
    dot_general x1, matrix products, weight_terms(): jnp.einsum('rjcf,rjcd->jfd', grad_up, inputs, preferred_element_type=jnp....  13.5 us
  transfers between devices with their start and end apart: 10, of which 6 were waited for; matrix products, arithmetic and copies ran while one was open for 24% of the time, Pallas kernels for 0%

profile of v1, /device:TPU:0, one launch (start us, length us, event | category | flops | bytes accessed | tf_op | source)
XLA Modules:
  0.0 286.8 jit_solution(2419793541942767327)
XLA Ops:
  7.2 0.9 copy.71
  8.4 0.2 select_reduce_fusion.1
  8.8 0.7 multiply_add_fusion
  9.4 0.1 copy.73
  9.5 0.1 fusion.36
  9.7 0.3 convolution_convert_fusion
  10.0 0.1 reshape.56
  10.1 0.4 copy.77
  10.5 11.6 %all_to_all.15 = bf16[4,2,6,4096]{3,1,2,0:T(2,128)(2,1)} all-to-all(bf16[4,2,6,4096]{3,1,2,0:T(2,128)(2,1)S(1)} %copy.77), channel_id=1, replica_groups=mesh['dp'=2,'expert'=4,'sample'=4] {'expert'}, dimensions={0} | all-to-all | bytes 786432 | tf_op jit(solution)/shard_map/all_to_all | solution.py:85
  22.8 5.3 %collective-permute-start.2 = (f32[1,1]{1,0:T(1,128)}, f32[1,1]{1,0:T(1,128)}, u32[]{:S(2)}, u32[]{:S(2)}) collective-permute-start(f32[1,1]{1,0:T(1,128)} %mul.63), channel_id=1, source_target_pairs={{0,3},{1,0},{2,1},{3,2},{4,7},{5,4},{6,5},{7,6},{8,11},{9,8},{10,9... | collective-permute-start | bytes 20 | tf_op jit(solution)/shard_map/ppermute | solution.py:57
  28.2 1.3 collective-permute-start.1
  29.5 2.3 collective-permute-start
  32.4 2.5 collective-permute-done
  36.9 0.1 copy.74
  37.2 0.3 fusion.15
  37.5 0.1 reshape.55
  37.6 0.4 copy.75
  38.0 10.5 %all_to_all.16 = bf16[4,2,6,4096]{3,1,2,0:T(2,128)(2,1)} all-to-all(bf16[4,2,6,4096]{3,1,2,0:T(2,128)(2,1)S(1)} %copy.75), channel_id=1, replica_groups=mesh['dp'=2,'expert'=4,'sample'=4] {'expert'}, dimensions={0} | all-to-all | bytes 786432 | tf_op jit(solution)/shard_map/all_to_all | solution.py:88
  48.6 34.4 %all-gather.5.cloned.1.call-done = bf16[32,2,6,4096]{3,1,2,0:T(2,128)(2,1)} async-done(((bf16[4,2,6,4096]{3,1,2,0:T(2,128)(2,1)}), bf16[32,2,6,4096]{3,1,2,0:T(2,128)(2,1)}) %all-gather.5.cloned.1.call-update) | async-done | bytes 3145744 | tf_op jit(solution)/shard_map/all_gather | solution.py:93
  83.0 15.3 %fusion.2 = f32[2,32,6,1024]{3,1,2,0:T(8,128)} fusion(bf16[2,1024,4096]{2,1,0:T(8,128)(2,1)} %param.15, bf16[32,2,6,4096]{3,1,2,0:T(2,128)(2,1)} %all-gather.5.cloned.1.call-done), kind=kOutput, calls=%fused_computation.5 | convolution fusion | flops 3221225472 | bytes 21495808 | tf_op jit(solution)/shard_map/rjcd,jfd->rjcf/dot_general | solution.py:15
  98.3 14.6 %fusion.8 = f32[2,32,6,1024]{3,1,2,0:T(8,128)} fusion(bf16[2,1024,4096]{2,1,0:T(8,128)(2,1)} %param.16, bf16[32,2,6,4096]{3,1,2,0:T(2,128)(2,1)S(1)} %copy-done.10), kind=kOutput, calls=%fused_computation.11 | convolution fusion | flops 3221225472 | bytes 21495808 | tf_op jit(solution)/shard_map/rjcd,jfd->rjcf/dot_general | solution.py:16
  112.8 31.0 %all-gather.3.cloned.1.call-done = bf16[32,2,6,4096]{3,1,2,0:T(2,128)(2,1)} async-done(((bf16[4,2,6,4096]{3,1,2,0:T(2,128)(2,1)}), bf16[32,2,6,4096]{3,1,2,0:T(2,128)(2,1)}) %all-gather.3.cloned.1.call-update) | async-done | bytes 3145744 | tf_op jit(solution)/shard_map/all_gather | solution.py:94
  143.8 15.0 %fusion.31 = (bf16[32,2,6,1024]{3,0,2,1:T(8,128)(2,1)S(1)}, bf16[32,2,6,1024]{3,0,2,1:T(8,128)(2,1)S(1)}) fusion(f32[2,32,6,1024]{3,1,2,0:T(8,128)} %fusion.2, f32[2,32,6,1024]{3,1,2,0:T(8,128)} %fusion.8, bf16[2,1024,4096]{2,1,0:T(8,128)(2,1)} %param.17, bf16[32,2,6,4096]{3,1,2,0:T(2,128)(2,1)} %all-gather.3.cloned.1.call-done), kind=kOutput, calls=%fused_computation.41 | convolution fusion | flops 3226337280 | bytes 24641536 | tf_op jit(solution)/shard_map/rjcd,jfd->rjcf/dot_general | solution.py:19
  158.8 8.4 %fusion = f32[2,32,6,4096]{3,1,2,0:T(8,128)S(1)} fusion(bf16[32,2,6,1024]{3,0,2,1:T(8,128)(2,1)S(1)} %get-tuple-element.5, bf16[2,1024,4096]{2,1,0:T(8,128)(2,1)} %param.15), kind=kOutput, calls=%fused_computation.3 | convolution fusion | flops 3221225472 | bytes 23855104 | tf_op jit(solution)/shard_map/rjcf,jfd->rjcd/dot_general | solution.py:35
  167.2 9.5 %fusion.12 = bf16[32,2,6,4096]{3,0,2,1:T(8,128)(2,1)S(1)} fusion(f32[2,32,6,4096]{3,1,2,0:T(8,128)S(1)} %fusion, bf16[32,2,6,1024]{3,0,2,1:T(8,128)(2,1)S(1)} %get-tuple-element.4, bf16[2,1024,4096]{2,1,0:T(8,128)(2,1)} %param.16), kind=kOutput, calls=%fused_computation.14 | convolution fusion | flops 3224371200 | bytes 27000832 | tf_op jit(solution)/shard_map/rjcf,jfd->rjcd/dot_general | solution.py:36
  176.7 3.8 %copy.80 = bf16[32,2,6,4096]{3,2,1,0:T(8,128)(2,1)} copy(bf16[32,2,6,4096]{3,0,2,1:T(8,128)(2,1)S(1)} %fusion.12) | data formatting | bytes 6291456 | tf_op jit(solution)/shard_map/convert_element_type | solution.py:100
  180.5 4.2 %reshape.57 = bf16[2,4,48,4096]{3,2,1,0:T(8,128)(2,1)S(1)} reshape(bf16[32,2,6,4096]{3,2,1,0:T(8,128)(2,1)} %copy.80) | data formatting | bytes 6291456 | tf_op jit(solution)/shard_map/reshape | solution.py:102
  184.7 0.1 dynamic-slice_bitcast_fusion
  184.8 0.6 collective-permute-start.3
  185.4 1.1 copy-done.11
  186.6 11.0 %bitcast_convert_fusion = bf16[2,1024,4096]{2,1,0:T(8,128)(2,1)} fusion(bf16[32,2,6,4096]{3,1,2,0:T(2,128)(2,1)S(1)} %copy-done.11, f32[2,32,6,1024]{3,1,2,0:T(8,128)} %fusion.8, f32[2,32,6,1024]{3,1,2,0:T(8,128)} %fusion.2), kind=kOutput, calls=%fused_computation | convolution fusion | flops 3231973376 | bytes 23068672 | tf_op jit(solution)/shard_map/rjcf,rjcd->jfd/dot_general | solution.py:30
  197.6 21.6 %collective-permute-done.3 = bf16[4,48,4096]{2,1,0:T(8,128)(2,1)S(1)} collective-permute-done((bf16[4,48,4096]{2,1,0:T(8,128)(2,1)S(1)}, bf16[4,48,4096]{2,1,0:T(8,128)(2,1)S(1)}, u32[]{:S(2)}, u32[]{:S(2)}) %collective-permute-start.3) | collective-permute-done | bytes 1572896 | tf_op jit(solution)/shard_map/ppermute | solution.py:47
  219.2 0.5 fusion.16
  219.8 1.1 copy-done.2
  221.0 1.8 collective-permute-start.4
  222.9 2.3 collective-permute-start.6
  225.1 1.0 collective-permute-start.5
  226.1 13.5 %bitcast_convert_fusion.1 = bf16[2,1024,4096]{2,1,0:T(8,128)(2,1)} fusion(bf16[32,2,6,1024]{3,0,2,1:T(8,128)(2,1)} %copy-done.5, bf16[32,2,6,4096]{3,1,2,0:T(2,128)(2,1)} %all-gather.5.cloned.1.call-done), kind=kOutput, calls=%fused_computation.1 | convolution fusion | flops 3229614080 | bytes 20709376 | tf_op jit(solution)/shard_map/rjcf,rjcd->jfd/dot_general | solution.py:29
  239.6 1.2 collective-permute-done.6
  240.8 17.0 %collective-permute-done.5 = bf16[48,4096]{1,0:T(8,128)(2,1)S(1)} collective-permute-done((bf16[48,4096]{1,0:T(8,128)(2,1)S(1)}, bf16[48,4096]{1,0:T(8,128)(2,1)S(1)}, u32[]{:S(2)}, u32[]{:S(2)}) %collective-permute-start.5) | collective-permute-done | bytes 393248 | tf_op jit(solution)/shard_map/ppermute | solution.py:47
  257.8 1.2 fusion.35
  259.0 0.1 reshape.58
  259.2 1.2 copy.81
  260.3 3.5 %all-to-all-start.2 = ((bf16[4,2,6,4096]{3,1,2,0:T(2,128)(2,1)}), bf16[4,2,6,4096]{3,1,2,0:T(2,128)(2,1)S(1)}, u32[]{:S(2)}, u32[]{:S(2)}) async-start(bf16[4,2,6,4096]{3,1,2,0:T(2,128)(2,1)} %copy.81), calls=%async_computation.2 | async-start | bytes 786432 | tf_op jit(solution)/shard_map/all_to_all | solution.py:104
  263.8 14.7 %bitcast_convert_fusion.2 = bf16[2,1024,4096]{2,1,0:T(8,128)(2,1)} fusion(bf16[32,2,6,1024]{3,0,2,1:T(8,128)(2,1)S(1)} %copy-done.4, bf16[32,2,6,4096]{3,1,2,0:T(2,128)(2,1)} %all-gather.5.cloned.1.call-done), kind=kOutput, calls=%fused_computation.2 | convolution fusion | flops 3229614080 | bytes 20709376 | tf_op jit(solution)/shard_map/rjcf,rjcd->jfd/dot_general | solution.py:28
  278.5 0.2 copy.82
  278.7 0.1 reshape.59
  278.9 0.9 convolution_convert_fusion.1
  (41 shorter events, 0.9 us)
Async XLA Ops:
  7.2 2.5 copy-start
  7.2 29.7 %copy-start.9 = (f32[20,2]{0,1:T(2,128)S(1)}, f32[20,2]{0,1:T(2,128)}, u32[]{:S(2)}) copy-start(f32[20,2]{0,1:T(2,128)} %param.12) | copy-start | bytes 484
  7.2 30.0 %copy-start.6 = (bf16[20,4096]{1,0:T(8,128)(2,1)S(1)}, bf16[20,4096]{1,0:T(8,128)(2,1)}, u32[]{:S(2)}) copy-start(bf16[20,4096]{1,0:T(8,128)(2,1)} %param.10) | copy-start | bytes 491524
  7.2 75.8 %all-gather.5.cloned.1.call-start = ((), (), s32[]{:S(2)}) async-start(), calls=%async_computation.4 | async-start | bytes 3538944 | tf_op jit(solution)/shard_map/all_gather | solution.py:93
  9.7 38.9 %copy-start.7 = (bf16[20,48]{1,0:T(8,128)(2,1)}, bf16[20,48]{1,0:T(8,128)(2,1)S(1)}, u32[]{:S(2)}) copy-start(bf16[20,48]{1,0:T(8,128)(2,1)S(1)} %fusion.36) | copy-start | bytes 5764
  22.1 121.7 %all-gather.3.cloned.1.call-start = ((), (), s32[]{:S(2)}) async-start(), calls=%async_computation.3 | async-start | bytes 3538944 | tf_op jit(solution)/shard_map/all_gather | solution.py:94
  22.8 13.3 %collective-permute-start.2 = (f32[1,1]{1,0:T(1,128)}, f32[1,1]{1,0:T(1,128)}, u32[]{:S(2)}, u32[]{:S(2)}) collective-permute-start(f32[1,1]{1,0:T(1,128)} %mul.63), channel_id=1, source_target_pairs={{0,3},{1,0},{2,1},{3,2},{4,7},{5,4},{6,5},{7,6},{8,11},{9,8},{10,9... | collective-permute-start | bytes 20 | tf_op jit(solution)/shard_map/ppermute | solution.py:57
  28.2 7.3 %collective-permute-start.1 = (f32[1,1]{1,0:T(1,128)}, f32[1,1]{1,0:T(1,128)}, u32[]{:S(2)}, u32[]{:S(2)}) collective-permute-start(f32[1,1]{1,0:T(1,128)} %mul.63), channel_id=1, source_target_pairs={{0,2},{1,3},{2,0},{3,1},{4,6},{5,7},{6,4},{7,5},{8,10},{9,11},{10,... | collective-permute-start | bytes 20 | tf_op jit(solution)/shard_map/ppermute | solution.py:57
  29.5 5.5 %collective-permute-start = (f32[1,1]{1,0:T(1,128)}, f32[1,1]{1,0:T(1,128)}, u32[]{:S(2)}, u32[]{:S(2)}) collective-permute-start(f32[1,1]{1,0:T(1,128)} %mul.63), channel_id=1, source_target_pairs={{0,1},{1,2},{2,3},{3,0},{4,5},{5,6},{6,7},{7,4},{8,9},{9,10},{10,1... | collective-permute-start | bytes 20 | tf_op jit(solution)/shard_map/ppermute | solution.py:57
  83.0 15.3 %copy-start.10 = (bf16[32,2,6,4096]{3,1,2,0:T(2,128)(2,1)S(1)}, bf16[32,2,6,4096]{3,1,2,0:T(2,128)(2,1)}, u32[]{:S(2)}) copy-start(bf16[32,2,6,4096]{3,1,2,0:T(2,128)(2,1)} %all-gather.5.cloned.1.call-done) | copy-start | bytes 9437188
  158.8 8.4 %copy-start.3 = (bf16[32,2,6,1024]{3,0,2,1:T(8,128)(2,1)}, bf16[32,2,6,1024]{3,0,2,1:T(8,128)(2,1)S(1)}, u32[]{:S(2)}) copy-start(bf16[32,2,6,1024]{3,0,2,1:T(8,128)(2,1)S(1)} %get-tuple-element.5) | copy-start | bytes 2359300
  158.8 8.4 %copy-start.5 = (bf16[32,2,6,1024]{3,0,2,1:T(8,128)(2,1)}, bf16[32,2,6,1024]{3,0,2,1:T(8,128)(2,1)S(1)}, u32[]{:S(2)}) copy-start(bf16[32,2,6,1024]{3,0,2,1:T(8,128)(2,1)S(1)} %get-tuple-element.4) | copy-start | bytes 2359300
  184.7 1.9 copy-start.11
  184.8 34.4 %collective-permute-start.3 = (bf16[4,48,4096]{2,1,0:T(8,128)(2,1)S(1)}, bf16[4,48,4096]{2,1,0:T(8,128)(2,1)S(1)}, u32[]{:S(2)}, u32[]{:S(2)}) collective-permute-start(bf16[4,48,4096]{2,1,0:T(8,128)(2,1)S(1)} %dynamic-slice_bitcast_fusion), channel_id=1, source_target_pairs={{0,16},{16,0},{1,17},{17,1},{2,18},{18,2},{3,19},{19,3},{4,20},{20... | collective-permute-start | bytes 4718600 | tf_op jit(solution)/shard_map/ppermute | solution.py:47
  219.8 1.1 copy-start.2
  221.0 18.6 %collective-permute-start.4 = (bf16[48,4096]{1,0:T(8,128)(2,1)S(1)}, bf16[48,4096]{1,0:T(8,128)(2,1)S(1)}, u32[]{:S(2)}, u32[]{:S(2)}) collective-permute-start(bf16[48,4096]{1,0:T(8,128)(2,1)S(1)} %get-tuple-element.6), channel_id=1, source_target_pairs={{0,1},{1,2},{2,3},{3,0},{4,5},{5,6},{6,7},{7,4},{8,9},{9,10},{10,1... | collective-permute-start | bytes 1179656 | tf_op jit(solution)/shard_map/ppermute | solution.py:47
  222.9 18.0 %collective-permute-start.6 = (bf16[48,4096]{1,0:T(8,128)(2,1)S(1)}, bf16[48,4096]{1,0:T(8,128)(2,1)S(1)}, u32[]{:S(2)}, u32[]{:S(2)}) collective-permute-start(bf16[48,4096]{1,0:T(8,128)(2,1)S(1)} %get-tuple-element.7), channel_id=1, source_target_pairs={{0,3},{1,0},{2,1},{3,2},{4,7},{5,4},{6,5},{7,6},{8,11},{9,8},{10,9... | collective-permute-start | bytes 1179656 | tf_op jit(solution)/shard_map/ppermute | solution.py:47
  225.1 32.7 %collective-permute-start.5 = (bf16[48,4096]{1,0:T(8,128)(2,1)S(1)}, bf16[48,4096]{1,0:T(8,128)(2,1)S(1)}, u32[]{:S(2)}, u32[]{:S(2)}) collective-permute-start(bf16[48,4096]{1,0:T(8,128)(2,1)S(1)} %get-tuple-element.8), channel_id=1, source_target_pairs={{0,2},{1,3},{2,0},{3,1},{4,6},{5,7},{6,4},{7,5},{8,10},{9,11},{10,... | collective-permute-start | bytes 1179656 | tf_op jit(solution)/shard_map/ppermute | solution.py:47
  239.6 24.2 %copy-start.4 = (bf16[32,2,6,1024]{3,0,2,1:T(8,128)(2,1)S(1)}, bf16[32,2,6,1024]{3,0,2,1:T(8,128)(2,1)}, u32[]{:S(2)}) copy-start(bf16[32,2,6,1024]{3,0,2,1:T(8,128)(2,1)} %copy-done.3) | copy-start | bytes 2359300
  260.3 18.2 %all-to-all-start.2 = ((bf16[4,2,6,4096]{3,1,2,0:T(2,128)(2,1)}), bf16[4,2,6,4096]{3,1,2,0:T(2,128)(2,1)S(1)}, u32[]{:S(2)}, u32[]{:S(2)}) async-start(bf16[4,2,6,4096]{3,1,2,0:T(2,128)(2,1)} %copy.81), calls=%async_computation.2 | async-start | bytes 786432 | tf_op jit(solution)/shard_map/all_to_all | solution.py:104
  263.8 15.1 %copy-start.8 = (bf16[20,48]{1,0:T(8,128)(2,1)S(1)}, bf16[20,48]{1,0:T(8,128)(2,1)}, u32[]{:S(2)}) copy-start(bf16[20,48]{1,0:T(8,128)(2,1)} %copy-done.7) | copy-start | bytes 5764
  263.8 15.9 %copy-start.1 = (bf16[20,4096]{1,0:T(8,128)(2,1)S(1)}, bf16[20,4096]{1,0:T(8,128)(2,1)}, u32[]{:S(2)}) copy-start(bf16[20,4096]{1,0:T(8,128)(2,1)} %param.9) | copy-start | bytes 491524
Sparse Core Ops, SparseCore 0:
  22.3 60.6 all-gather.4
  85.1 58.6 all-gather.2
